TPU v7x, 32 devices: a whole 2x2x4 slice. The times are simulated.
32 devices in a mesh: dp: 4 (over y, x), seq: 2 (over core), head: 4 (over z).
Axes of the slice: x: 2, y: 2, z: 4, core: 2. Of those that a mesh axis runs over, the one named last changes fastest.
Arguments:
- q_lat: bfloat16 [3072, 8192], P(('dp', 'seq'), 'head'), may hold values from -160 to 160
- q_rope: bfloat16 [3072, 1024], P(('dp', 'seq'), 'head'), may hold values from -6 to 6
- grad_out: bfloat16 [3072, 8192], P(('dp', 'seq'), 'head'), may hold values from -6 to 6
- prefix_keys: bfloat16 [576, 512], P(None, 'seq'), may hold values from -6 to 6
- comp_lengths: int32 [3], replicated, may hold values from 128 to 1024, as said below
- prefix_len: int32 [1], replicated, may hold values from 65 to 512
Outputs:
- dq_lat: bfloat16 [3072, 8192], P(('dp', 'seq'), 'head')
- dq_rope: bfloat16 [3072, 1024], P(('dp', 'seq'), 'head')
- d_keys: float32 [576, 512], P(None, ('seq', 'head'))
Inputs may be any that keep to these rules, and one draw needn't show every extreme that they name: `comp_lengths`: each a multiple of 128.
All inputs are finite; a program needn't handle non-finite values.
Results may differ from a plain program's by a relative error of at most 0.0089.
Values may be sent and summed in bfloat16 or wider, within the bound.
A program may use at most 64 MiB of HBM per device.

v0:
```python
import jax
import jax.numpy as jnp
from jax import lax
from jax.sharding import PartitionSpec as P

DL = 512
DR = 64
CLEN = 1024
neg_value = -1e30


def on_device(q_lat, q_rope, grad_out, prefix_keys, comp_lengths, prefix_len):
    tok_rows = q_lat.shape[0]
    heads_here = q_lat.shape[1] // DL
    rows = tok_rows * heads_here
    scale = (DL + DR) ** (-0.5)
    tok_ids = lax.axis_index(("dp", "seq")) * tok_rows + jnp.arange(tok_rows, dtype=jnp.int32)
    comp_ids = tok_ids // CLEN
    table = jnp.arange(comp_lengths.shape[0], dtype=jnp.int32)
    length = jnp.sum(
        jnp.where(comp_ids[:, None] == table[None, :], comp_lengths[None, :], 0), axis=1
    )
    valid = tok_ids % CLEN < length
    query_lat = q_lat.reshape(rows, DL)
    query_rope = q_rope.reshape(rows, DR)
    upstream = jnp.where(
        jnp.repeat(valid, heads_here)[:, None],
        grad_out.reshape(rows, DL),
        jnp.zeros((), jnp.bfloat16),
    )
    limit = prefix_len[0]
    total_keys = prefix_keys.shape[1] * lax.axis_size("seq")
    contract_last = (((1,), (1,)), ((), ()))
    contract_first = (((0,), (0,)), ((), ()))

    def scores_of(piece):
        key_lat = piece[:DL]
        key_rope = piece[DL:]
        scores = (
            jnp.dot(query_lat, key_lat, preferred_element_type=jnp.float32)
            + jnp.dot(query_rope, key_rope, preferred_element_type=jnp.float32)
        ) * scale
        keep = jnp.arange(piece.shape[1], dtype=jnp.int32) < limit
        dprob = jnp.dot(upstream, key_lat, preferred_element_type=jnp.float32)
        return (key_lat, key_rope, scores, keep[None, :], dprob)

    def make_backward(peak, total, delta):

        def backward_step(carry, piece, start):
            key_lat, key_rope, scores, keep, dprob = scores_of(piece)
            prob = jnp.where(
                keep,
                jnp.exp(jnp.where(keep, scores, neg_value) - peak[:, None]) / total[:, None],
                0.0,
            )
            dscore = prob * (dprob - delta[:, None])
            prob_b = prob.astype(jnp.bfloat16)
            dscore_b = dscore.astype(jnp.bfloat16)
            grad_lat = lax.dot_general(
                dscore_b, key_lat, contract_last, preferred_element_type=jnp.float32
            )
            grad_rope = lax.dot_general(
                dscore_b, key_rope, contract_last, preferred_element_type=jnp.float32
            )
            term_lat = lax.dot_general(
                upstream, prob_b, contract_first, preferred_element_type=jnp.float32
            ) + scale * lax.dot_general(
                query_lat, dscore_b, contract_first, preferred_element_type=jnp.float32
            )
            term_rope = scale * lax.dot_general(
                query_rope, dscore_b, contract_first, preferred_element_type=jnp.float32
            )
            update = jnp.concatenate([term_lat, term_rope], axis=0)
            return (grad_lat, grad_rope, update)

        return backward_step

    grads_init = (
        jnp.zeros((rows, DL), jnp.float32),
        jnp.zeros((rows, DR), jnp.float32),
        jnp.zeros((DL + DR, total_keys), jnp.float32),
    )
    peak = jnp.full((rows,), neg_value, jnp.float32)
    total = jnp.zeros((rows,), jnp.float32)
    key_lat, key_rope, scores, keep, dprob = scores_of(
        lax.all_gather(prefix_keys, "seq", axis=1, tiled=True)
    )
    masked = jnp.where(keep, scores, neg_value)
    new_peak = jnp.maximum(peak, jnp.max(masked, axis=1))
    expo = jnp.where(keep, jnp.exp(masked - new_peak[:, None]), 0.0)
    peak = new_peak
    total = jnp.sum(expo, axis=1)
    weighted = jnp.sum(expo * dprob, axis=1)
    backward_step = make_backward(peak, total, weighted / total)
    grad_lat, grad_rope, key_grads = backward_step(
        grads_init, lax.all_gather(prefix_keys, "seq", axis=1, tiled=True), jnp.int32(0)
    )
    by_seq = lax.psum_scatter(key_grads, "seq", scatter_dimension=1, tiled=True)
    portion = lax.psum_scatter(by_seq, "head", scatter_dimension=1, tiled=True)
    d_keys = lax.psum(portion, "dp")
    dq_lat = (scale * grad_lat).astype(jnp.bfloat16).reshape(tok_rows, heads_here * DL)
    dq_rope = (scale * grad_rope).astype(jnp.bfloat16).reshape(tok_rows, heads_here * DR)
    return (dq_lat, dq_rope, d_keys)


def solution(mesh):
    in_specs = (
        P(("dp", "seq"), "head"),
        P(("dp", "seq"), "head"),
        P(("dp", "seq"), "head"),
        P(None, "seq"),
        P(),
        P(),
    )
    out_specs = (P(("dp", "seq"), "head"), P(("dp", "seq"), "head"), P(None, ("seq", "head")))
    return jax.shard_map(
        on_device, mesh=mesh, in_specs=in_specs, out_specs=out_specs, check_vma=False
    )
```

profile of v0, /device:TPU:0, one launch (start us, length us, event | category | flops | bytes accessed | tf_op | source)
XLA Modules:
  0.0 119.2 jit_solution(12004956962151974699)
XLA Ops:
  7.9 0.7 select_reduce_fusion.1
  8.9 1.2 reshape.56
  10.1 2.6 %all_gather.4 = bf16[576,512]{1,0:T(8,128)(2,1)S(1)} all-gather(bf16[576,256]{1,0:T(8,128)(2,1)} %param.9), channel_id=1, replica_groups=mesh['dp'=4,'seq'=2,'head'=4] {'seq'}, dimensions={1}, use_global_device_ids=true | all-gather | bytes 884736 | tf_op jit(solution)/shard_map/all_gather | solution.py:96
  12.7 2.9 %reshape.55 = bf16[1536,512]{1,0:T(8,128)(2,1)S(1)} reshape(bf16[384,2048]{1,0:T(8,128)(2,1)} %param.6) | data formatting | bytes 3145728 | tf_op jit(solution)/shard_map/reshape | solution.py:24
  15.6 3.7 %reshape.57 = bf16[1536,512]{1,0:T(8,128)(2,1)} reshape(bf16[384,2048]{1,0:T(8,128)(2,1)} %param.8) | data formatting | bytes 3145728 | tf_op jit(solution)/shard_map/reshape | solution.py:28
  19.4 1.0 fusion.12
  20.4 0.7 fusion.22
  21.2 0.6 copy-done.2
  21.8 1.6 %select_reduce_fusion = (f32[1536]{0:T(1024)S(1)}, f32[1536]{0:T(1024)S(1)}, f32[1536,512]{0,1:T(8,128)S(1)}) fusion(f32[1536,512]{0,1:T(8,128)S(1)} %get-tuple-element.18, f32[1536]{0:T(1024)S(1)} %broadcast_maximum_fusion, pred[512]{0:T(512)(128)(4,1)S(1)} %iota_compare_fusion.1, bf16[576,512]{1,0:T(8,128)(2,1)S(1)} %all_gather.4, ...), kind=kOutput, calls=%fused_computation.9 | convolution fusion | flops 810021888 | bytes 8411648 | tf_op jit(solution)/shard_map/dot_general | solution.py:44
  23.4 1.5 %fusion.4 = f32[512,512]{1,0:T(8,128)S(1)} fusion(bf16[1536,512]{1,0:T(8,128)(2,1)S(1)} %copy-done.2, pred[1536]{0:T(1024)(128)(4,1)S(1)} %broadcast_in_dim.74, f32[1536,512]{0,1:T(8,128)S(1)} %get-tuple-element.18, f32[1536]{0:T(1024)S(1)} %get-tuple-element.15, f32[1536]{0:T(1024)S(1)} %broadcast_maximum_fusion, pred[512]{0:T(512)(128)(4,1)S(1)} %iota_compare_fusion.1), kind=kOutput, calls=%fused_computation.12 | convolution fusion | flops 809238528 | bytes 5781504 | tf_op jit(solution)/shard_map/dot_general | solution.py:65
  24.9 0.9 multiply_convert_fusion
  26.4 1.0 fusion.7
  27.4 1.1 pad_maximum_fusion
  28.6 11.2 %reduce-scatter.5.cloned.1.call-done = f32[576,256]{1,0:T(8,128)} async-done(((f32[576,512]{1,0:T(8,128)}), f32[576,256]{1,0:T(8,128)}) %reduce-scatter.5.cloned.1.call-update) | async-done | bytes 589840 | tf_op jit(solution)/shard_map/reduce_scatter | solution.py:98
  39.8 2.1 %copy.24 = f32[576,256]{0,1:T(8,128)} copy(f32[576,256]{1,0:T(8,128)} %reduce-scatter.5.cloned.1.call-done) | data formatting | bytes 1179648
  42.0 2.1 %fusion.2 = bf16[1536,512]{0,1:T(8,128)(2,1)} fusion(bf16[1536,512]{0,1:T(8,128)(2,1)S(1)} %multiply_convert_fusion, bf16[576,512]{1,0:T(8,128)(2,1)S(1)} %copy-done.1), kind=kOutput, calls=%fused_computation.8 | convolution fusion | flops 806879232 | bytes 3670016 | tf_op jit(solution)/shard_map/dot_general | solution.py:59
  44.1 1.7 %copy.20 = bf16[1536,512]{1,0:T(8,128)(2,1)S(1)} copy(bf16[1536,512]{0,1:T(8,128)(2,1)} %fusion.2) | data formatting | bytes 3145728 | tf_op jit(solution)/shard_map/convert_element_type | solution.py:101
  45.8 2.2 %reshape.58 = bf16[384,2048]{1,0:T(8,128)(2,1)} reshape(bf16[1536,512]{1,0:T(8,128)(2,1)S(1)} %copy.20) | data formatting | bytes 3145728 | tf_op jit(solution)/shard_map/reshape | solution.py:101
  48.1 17.8 %reduce-scatter.7.cloned.1.call-done = f32[64,576]{1,0:T(8,128)} async-done(((f32[256,576]{1,0:T(8,128)}), f32[64,576]{1,0:T(8,128)}) %reduce-scatter.7.cloned.1.call-update) | async-done | bytes 147472
  65.9 1.8 %copy.25 = f32[576,64]{1,0:T(8,128)} copy(f32[576,64]{0,1:T(8,128)} %bitcast.19) | data formatting | bytes 294912
  67.7 1.2 %fusion.3 = bf16[1536,64]{0,1:T(8,128)(2,1)S(1)} fusion(bf16[1536,512]{0,1:T(8,128)(2,1)S(1)} %multiply_convert_fusion, bf16[576,512]{1,0:T(8,128)(2,1)} %copy-done), kind=kOutput, calls=%fused_computation.11 | convolution fusion | flops 100859904 | bytes 1835008 | tf_op jit(solution)/shard_map/dot_general | solution.py:62
  69.2 1.0 reshape.59
  70.1 40.8 %all-reduce.2.cloned.1.call-done = f32[576,64]{1,0:T(8,128)} async-done(((f32[576,64]{1,0:T(8,128)}), f32[576,64]{1,0:T(8,128)}) %all-reduce.2.cloned.1.call-update) | async-done | bytes 147472 | tf_op jit(solution)/shard_map/psum | solution.py:100
  110.9 1.8 %copy.22 = f32[576,64]{0,1:T(8,128)} copy(f32[576,64]{1,0:T(8,128)} %all-reduce.2.cloned.1.call-done) | data formatting | bytes 294912
  (20 shorter events, 1.3 us)
Async XLA Ops:
  7.2 32.6 %reduce-scatter.5.cloned.1.call-start = ((), (), s32[]{:S(2)}) async-start(), calls=%async_computation.2 | async-start | bytes 1769472 | tf_op jit(solution)/shard_map/reduce_scatter | solution.py:98
  12.7 8.5 %copy-start = (bf16[576,512]{1,0:T(8,128)(2,1)}, bf16[576,512]{1,0:T(8,128)(2,1)S(1)}, u32[]{:S(2)}) copy-start(bf16[576,512]{1,0:T(8,128)(2,1)S(1)} %all_gather.4) | copy-start | bytes 1769476
  20.4 1.4 %copy-start.2 = (bf16[1536,512]{1,0:T(8,128)(2,1)S(1)}, bf16[1536,512]{1,0:T(8,128)(2,1)}, u32[]{:S(2)}) copy-start(bf16[1536,512]{1,0:T(8,128)(2,1)} %reshape.57) | copy-start | bytes 4718596
  28.5 13.5 %copy-start.1 = (bf16[576,512]{1,0:T(8,128)(2,1)S(1)}, bf16[576,512]{1,0:T(8,128)(2,1)}, u32[]{:S(2)}) copy-start(bf16[576,512]{1,0:T(8,128)(2,1)} %copy-done) | copy-start | bytes 1769476
  28.5 37.4 %reduce-scatter.7.cloned.1.call-start = ((), (), s32[]{:S(2)}) async-start(), calls=%async_computation.4 | async-start | bytes 819200
  41.9 69.0 %all-reduce.2.cloned.1.call-start = ((), (), s32[]{:S(2)}) async-start(), calls=%async_computation.3 | async-start | bytes 589824 | tf_op jit(solution)/shard_map/psum | solution.py:100
Sparse Core Ops, SparseCore 0:
  28.6 11.0 reduce-scatter.4
  42.1 23.8 reduce-scatter.6
  68.9 41.9 all-reduce.1
where the time goes:
time: 120 us; the launch traced here: 119 us
  waiting for transfers between devices  69.9 us (58%)
  local copies, waits for them, and re-layouts  19.6 us (16%)
  between operations  14.5 us (12%)
  matrix products  9.83 us (8%)
  other arithmetic  2.74 us (2%)
  blocking collectives  2.56 us (2%)
    psum x1, waiting for transfers between devices, on_device(): d_keys = lax.psum(portion, 'dp')  40.8 us
    unnamed x4, waiting for transfers between devices  17.9 us
    reduce_scatter x1, waiting for transfers between devices, on_device(): by_seq = lax.psum_scatter(key_grads, 'seq', scatter_dimension=1, tiled=True)  11.2 us
    unnamed x9, local copies, waits for them, and re-layouts  6.33 us
    reshape x1, local copies, waits for them, and re-layouts, on_device(): grad_out.reshape(rows, DL)  3.73 us
    reshape x1, local copies, waits for them, and re-layouts, on_device(): query_lat = q_lat.reshape(rows, DL)  2.94 us
    all_gather x1, blocking collectives, on_device(): lax.all_gather(prefix_keys, 'seq', axis=1, tiled=True)  2.56 us
  transfers between devices with their start and end apart: 3, of which 3 were waited for; matrix products, arithmetic and copies ran while one was open for 7% of the time, Pallas kernels for 0%

commit v1 on v0

--- a/solution.py
+++ b/solution.py
@@ -97,7 +97,7 @@
     )
     by_seq = lax.psum_scatter(key_grads, "seq", scatter_dimension=1, tiled=True)
     portion = lax.psum_scatter(by_seq, "head", scatter_dimension=1, tiled=True)
-    d_keys = lax.psum(portion, "dp")
+    d_keys = jnp.sum(lax.all_gather(portion, "dp"), axis=0)
     dq_lat = (scale * grad_lat).astype(jnp.bfloat16).reshape(tok_rows, heads_here * DL)
     dq_rope = (scale * grad_rope).astype(jnp.bfloat16).reshape(tok_rows, heads_here * DR)
     return (dq_lat, dq_rope, d_keys)

time: 120 us -> 86.6 us (0.72)
  waiting for transfers between devices: 69.9 us -> 26.7 us
  blocking collectives: 2.56 us -> 14 us
  local copies, waits for them, and re-layouts: 19.6 us -> 17.2 us
    psum x1 -> x0, waiting for transfers between devices: 40.8 us -> none  [on_device(): d_keys = lax.psum(portion, 'dp')]
    all_gather x0 -> x1, blocking collectives: none -> 11.4 us  [on_device(): d_keys = jnp.sum(lax.all_gather(portion, 'dp'), axis=0)]
    unnamed x4 -> x3, waiting for transfers between devices: 17.9 us -> 15.5 us
    unnamed x9, local copies, waits for them, and re-layouts: 6.33 us -> 3.98 us
  transfers between devices with their start and end apart: 3 -> 2, of which waited for: 3 -> 2; matrix products, arithmetic and copies ran while one was open for 7% -> 10% of each run, Pallas kernels for 0% -> 0%
where the time goes in v1:
time: 86.6 us; the launch traced here: 86.1 us
  waiting for transfers between devices  26.7 us (31%)
  local copies, waits for them, and re-layouts  17.2 us (20%)
  between operations  14.8 us (17%)
  blocking collectives  14 us (16%)
  matrix products  9.83 us (11%)
  other arithmetic  3.44 us (4%)
    unnamed x3, waiting for transfers between devices  15.5 us
    all_gather x1, blocking collectives, on_device(): d_keys = jnp.sum(lax.all_gather(portion, 'dp'), axis=0)  11.4 us
    reduce_scatter x1, waiting for transfers between devices, on_device(): by_seq = lax.psum_scatter(key_grads, 'seq', scatter_dimension=1, tiled=True)  11.2 us
    unnamed x9, local copies, waits for them, and re-layouts  3.98 us
    reshape x1, local copies, waits for them, and re-layouts, on_device(): grad_out.reshape(rows, DL)  3.73 us
    reshape x1, local copies, waits for them, and re-layouts, on_device(): query_lat = q_lat.reshape(rows, DL)  2.94 us
    all_gather x1, blocking collectives, on_device(): lax.all_gather(prefix_keys, 'seq', axis=1, tiled=True)  2.56 us
    reshape x1, local copies, waits for them, and re-layouts, on_device(): (scale * grad_lat).astype(jnp.bfloat16).reshape(tok_rows, heads_here * DL)  2.23 us
  transfers between devices with their start and end apart: 2, of which 2 were waited for; matrix products, arithmetic and copies ran while one was open for 10% of the time, Pallas kernels for 0%

profile of v1, /device:TPU:0, one launch (start us, length us, event | category | flops | bytes accessed | tf_op | source)
XLA Modules:
  0.0 86.1 jit_solution(5987256369145521647)
XLA Ops:
  7.9 0.7 select_reduce_fusion.1
  8.9 1.2 %reshape.56 = bf16[1536,64]{1,0:T(8,128)(2,1)S(1)} reshape(bf16[384,256]{1,0:T(8,128)(2,1)} %param.7) | data formatting | bytes 393216 | tf_op jit(solution)/shard_map/reshape | solution.py:25
  10.1 2.6 %all_gather.10 = bf16[576,512]{1,0:T(8,128)(2,1)S(1)} all-gather(bf16[576,256]{1,0:T(8,128)(2,1)} %param.9), channel_id=1, replica_groups=mesh['dp'=4,'seq'=2,'head'=4] {'seq'}, dimensions={1}, use_global_device_ids=true | all-gather | bytes 884736 | tf_op jit(solution)/shard_map/all_gather | solution.py:96
  12.7 2.9 %reshape.55 = bf16[1536,512]{1,0:T(8,128)(2,1)S(1)} reshape(bf16[384,2048]{1,0:T(8,128)(2,1)} %param.6) | data formatting | bytes 3145728 | tf_op jit(solution)/shard_map/reshape | solution.py:24
  15.6 3.7 %reshape.57 = bf16[1536,512]{1,0:T(8,128)(2,1)} reshape(bf16[384,2048]{1,0:T(8,128)(2,1)} %param.8) | data formatting | bytes 3145728 | tf_op jit(solution)/shard_map/reshape | solution.py:28
  19.4 1.0 %fusion.12 = f32[1536,512]{0,1:T(8,128)S(1)} fusion(bf16[1536,512]{1,0:T(8,128)(2,1)S(1)} %reshape.55, bf16[576,512]{1,0:T(8,128)(2,1)S(1)} %all_gather.10), kind=kOutput, calls=%fused_computation.24 | convolution fusion | flops 805306368 | bytes 5242880 | tf_op jit(solution)/shard_map/dot_general | solution.py:40
  20.4 0.7 fusion.22
  21.2 0.6 copy-done.2
  21.8 1.6 %select_reduce_fusion = (f32[1536]{0:T(1024)S(1)}, f32[1536]{0:T(1024)S(1)}, f32[1536,512]{0,1:T(8,128)S(1)}) fusion(f32[1536,512]{0,1:T(8,128)S(1)} %get-tuple-element.12, f32[1536]{0:T(1024)S(1)} %broadcast_maximum_fusion, pred[512]{0:T(512)(128)(4,1)S(1)} %iota_compare_fusion.1, bf16[576,512]{1,0:T(8,128)(2,1)S(1)} %all_gather.10, ...), kind=kOutput, calls=%fused_computation.9 | convolution fusion | flops 810021888 | bytes 8411648 | tf_op jit(solution)/shard_map/dot_general | solution.py:44
  23.4 1.5 %fusion.4 = f32[512,512]{1,0:T(8,128)S(1)} fusion(bf16[1536,512]{1,0:T(8,128)(2,1)S(1)} %copy-done.2, pred[1536]{0:T(1024)(128)(4,1)S(1)} %broadcast_in_dim.74, f32[1536,512]{0,1:T(8,128)S(1)} %get-tuple-element.12, f32[1536]{0:T(1024)S(1)} %get-tuple-element.9, f32[1536]{0:T(1024)S(1)} %broadcast_maximum_fusion, pred[512]{0:T(512)(128)(4,1)S(1)} %iota_compare_fusion.1), kind=kOutput, calls=%fused_computation.12 | convolution fusion | flops 809238528 | bytes 5781504 | tf_op jit(solution)/shard_map/dot_general | solution.py:65
  24.9 0.9 multiply_convert_fusion
  26.4 1.0 %fusion.7 = f32[512,512]{1,0:T(8,128)S(1)} fusion(f32[512,512]{1,0:T(8,128)S(1)} %fusion.4, bf16[1536,512]{0,1:T(8,128)(2,1)S(1)} %multiply_convert_fusion, bf16[1536,512]{1,0:T(8,128)(2,1)S(1)} %reshape.55), kind=kOutput, calls=%fused_computation.17 | convolution fusion | flops 805830656 | bytes 5242880 | tf_op jit(solution)/shard_map/dot_general | solution.py:67
  27.4 1.1 %pad_maximum_fusion = f32[576,512]{1,0:T(8,128)} fusion(f32[64,512]{1,0:T(8,128)S(1)} %fusion.8, f32[512,512]{1,0:T(8,128)S(1)} %fusion.7), kind=kLoop, calls=%fused_computation.18 | loop fusion | flops 294912 | bytes 2359296 | tf_op jit(solution)/shard_map/concatenate | solution.py:73
  28.6 11.2 %reduce-scatter.5.cloned.1.call-done = f32[576,256]{1,0:T(8,128)} async-done(((f32[576,512]{1,0:T(8,128)}), f32[576,256]{1,0:T(8,128)}) %reduce-scatter.5.cloned.1.call-update) | async-done | bytes 589840 | tf_op jit(solution)/shard_map/reduce_scatter | solution.py:98
  39.8 2.1 %copy.26 = f32[576,256]{0,1:T(8,128)} copy(f32[576,256]{1,0:T(8,128)} %reduce-scatter.5.cloned.1.call-done) | data formatting | bytes 1179648
  41.9 2.1 %fusion.2 = bf16[1536,512]{0,1:T(8,128)(2,1)} fusion(bf16[1536,512]{0,1:T(8,128)(2,1)S(1)} %multiply_convert_fusion, bf16[576,512]{1,0:T(8,128)(2,1)S(1)} %copy-done.1), kind=kOutput, calls=%fused_computation.8 | convolution fusion | flops 806879232 | bytes 3670016 | tf_op jit(solution)/shard_map/dot_general | solution.py:59
  44.1 1.7 %copy.20 = bf16[1536,512]{1,0:T(8,128)(2,1)S(1)} copy(bf16[1536,512]{0,1:T(8,128)(2,1)} %fusion.2) | data formatting | bytes 3145728 | tf_op jit(solution)/shard_map/convert_element_type | solution.py:101
  45.8 2.2 %reshape.58 = bf16[384,2048]{1,0:T(8,128)(2,1)} reshape(bf16[1536,512]{1,0:T(8,128)(2,1)S(1)} %copy.20) | data formatting | bytes 3145728 | tf_op jit(solution)/shard_map/reshape | solution.py:101
  48.0 1.2 %fusion.3 = bf16[1536,64]{0,1:T(8,128)(2,1)S(1)} fusion(bf16[1536,512]{0,1:T(8,128)(2,1)S(1)} %multiply_convert_fusion, bf16[576,512]{1,0:T(8,128)(2,1)} %copy-done), kind=kOutput, calls=%fused_computation.11 | convolution fusion | flops 100859904 | bytes 1835008 | tf_op jit(solution)/shard_map/dot_general | solution.py:62
  49.5 1.0 %reshape.59 = bf16[384,256]{1,0:T(8,128)(2,1)} reshape(bf16[1536,64]{1,0:T(8,128)(2,1)S(1)} %copy.21) | data formatting | bytes 393216 | tf_op jit(solution)/shard_map/reshape | solution.py:102
  50.4 15.5 %reduce-scatter.7.cloned.1.call-done = f32[64,576]{1,0:T(8,128)} async-done(((f32[256,576]{1,0:T(8,128)}), f32[64,576]{1,0:T(8,128)}) %reduce-scatter.7.cloned.1.call-update) | async-done | bytes 147472
  65.9 1.1 %copy.27 = f32[576,64]{1,0:T(8,128)S(1)} copy(f32[576,64]{0,1:T(8,128)} %bitcast.21) | data formatting | bytes 294912
  67.1 11.4 %all-gather.1 = f32[4,576,64]{1,2,0:T(8,128)S(1)} all-gather(f32[1,576,64]{1,2,0:T(8,128)S(1)} %copy.22), channel_id=2, replica_groups=mesh['dp'=4,'seq'=2,'head'=4] {'dp'}, dimensions={0}, use_global_device_ids=true | all-gather | bytes 737280 | tf_op jit(solution)/shard_map/all_gather | solution.py:100
  78.5 0.7 reduce_sum.39
  (19 shorter events, 1.4 us)
Async XLA Ops:
  7.2 32.6 %reduce-scatter.5.cloned.1.call-start = ((), (), s32[]{:S(2)}) async-start(), calls=%async_computation.2 | async-start | bytes 1769472 | tf_op jit(solution)/shard_map/reduce_scatter | solution.py:98
  12.7 8.5 %copy-start = (bf16[576,512]{1,0:T(8,128)(2,1)}, bf16[576,512]{1,0:T(8,128)(2,1)S(1)}, u32[]{:S(2)}) copy-start(bf16[576,512]{1,0:T(8,128)(2,1)S(1)} %all_gather.10) | copy-start | bytes 1769476
  20.4 1.4 %copy-start.2 = (bf16[1536,512]{1,0:T(8,128)(2,1)S(1)}, bf16[1536,512]{1,0:T(8,128)(2,1)}, u32[]{:S(2)}) copy-start(bf16[1536,512]{1,0:T(8,128)(2,1)} %reshape.57) | copy-start | bytes 4718596
  28.5 13.4 %copy-start.1 = (bf16[576,512]{1,0:T(8,128)(2,1)S(1)}, bf16[576,512]{1,0:T(8,128)(2,1)}, u32[]{:S(2)}) copy-start(bf16[576,512]{1,0:T(8,128)(2,1)} %copy-done) | copy-start | bytes 1769476
  28.5 37.4 %reduce-scatter.7.cloned.1.call-start = ((), (), s32[]{:S(2)}) async-start(), calls=%async_computation.3 | async-start | bytes 819200
Sparse Core Ops, SparseCore 0:
  28.6 11.0 reduce-scatter.4
  42.1 23.8 reduce-scatter.6
